TPU v7x, 1024 devices: a whole 4x4x32 slice. The times are simulated.
1024 devices in a mesh: grp: 16 (over z_lo), cp: 64 (over y, x, z_hi, core).
Axes of the slice: x: 4, y: 4, z: 32 (z_hi: 2, z_lo: 16; z = z_hi * 16 + z_lo), core: 2. Of those that a mesh axis runs over, the one named last changes fastest.
Arguments:
- query_proj: bfloat16 [131072, 4096], P(('grp', 'cp')), may hold values from -6 to 6
- key_proj: bfloat16 [131072, 512], P(('grp', 'cp')), may hold values from -6 to 6
- value_projection: bfloat16 [131072, 512], P(('grp', 'cp')), may hold values from -6 to 6
- segment_ids: int32 [131072], P(('grp', 'cp')), may hold values from 0 to 511, never falling along the last dimension, each value on 1 to 1024 neighbouring positions
Outputs:
- attended: bfloat16 [131072, 4096], P(('grp', 'cp'))
Inputs may be any that keep to these rules, and one draw needn't show every extreme that they name: `segment_ids`: never falls along the stream; every document has 1 to 1024 tokens, and one has exactly 1024.
All inputs are finite; a program needn't handle non-finite values.
Results may differ from a plain program's by a relative error of at most 0.0034.
Values may be sent and summed in bfloat16 or wider, within the bound.
No kernel may reach another device: no remote copies, remote signals or barrier semaphores. Data moves between devices by JAX's collectives and lax.ppermute only.
A program may use at most 64 MiB of HBM per device.

v0:
```python
import math

import jax
import jax.numpy as jnp
from jax import lax
from jax.sharding import PartitionSpec as P

HEAD_WIDTH = 128
SPAN = 8


def passed_along(value, axis, steps):
    count = lax.axis_size(axis)
    first, last = (max(0, -steps), min(count, count - steps))
    return lax.ppermute(value, axis, [(source, source + steps) for source in range(first, last)])


def attend_window(query_rows, key_win, value_win, seg_query, seg_keys, pos_query, pos_keys):
    tok_rows = query_rows.shape[0]
    group_size = query_rows.shape[1] // key_win.shape[1]
    kv_count = key_win.shape[1] // HEAD_WIDTH
    score_scale = 1.0 / math.sqrt(HEAD_WIDTH)
    sub_heads = max(1, min(group_size, 512 // tok_rows))
    while group_size % sub_heads != 0:
        sub_heads = sub_heads - 1
    visible = (
        (seg_query[:, None] == seg_keys[None, :])
        & (pos_keys[None, :] <= pos_query[:, None])
        & (pos_keys[None, :] >= 0)
    )
    pieces_out = []
    for kv_head in range(kv_count):
        k_block = key_win[:, kv_head * HEAD_WIDTH : (kv_head + 1) * HEAD_WIDTH]
        v_block = value_win[:, kv_head * HEAD_WIDTH : (kv_head + 1) * HEAD_WIDTH]
        for sub_start in range(0, group_size, sub_heads):
            col_begin = (kv_head * group_size + sub_start) * HEAD_WIDTH
            q_block = query_rows[:, col_begin : col_begin + sub_heads * HEAD_WIDTH].reshape(
                tok_rows, sub_heads, HEAD_WIDTH
            )
            scores = (
                jnp.einsum("tgd,sd->tgs", q_block, k_block, preferred_element_type=jnp.float32)
                * score_scale
            )
            scores = jnp.where(visible[:, None, :], scores, -jnp.inf)
            row_max = jnp.max(scores, axis=2, keepdims=True)
            weights = jnp.exp(scores - row_max)
            row_total = jnp.sum(weights, axis=2, keepdims=True)
            probs = weights.astype(jnp.bfloat16)
            mixed = (
                jnp.einsum("tgs,sd->tgd", probs, v_block, preferred_element_type=jnp.float32)
                / row_total
            )
            pieces_out.append(mixed.reshape(tok_rows, sub_heads * HEAD_WIDTH).astype(jnp.bfloat16))
    return jnp.concatenate(pieces_out, axis=1)


def shards(query_proj, key_proj, value_projection, segment_ids):
    tok_rows = query_proj.shape[0]
    first_pos = (lax.axis_index("grp") * lax.axis_size("cp") + lax.axis_index("cp")) * tok_rows
    key_win, value_win, seg_win = (key_proj, value_projection, segment_ids)
    while key_win.shape[0] < (SPAN + 1) * tok_rows:
        reach_now = key_win.shape[0] // tok_rows
        missing = min(reach_now, SPAN + 1 - reach_now)
        send_from = key_win.shape[0] - missing * tok_rows
        earlier = passed_along(
            (key_win[send_from:], value_win[send_from:], seg_win[send_from:]),
            ("grp", "cp"),
            reach_now,
        )
        key_win = jnp.concatenate([earlier[0], key_win], 0)
        value_win = jnp.concatenate([earlier[1], value_win], 0)
        seg_win = jnp.concatenate([earlier[2], seg_win], 0)
    pos_query = first_pos + jnp.arange(tok_rows, dtype=jnp.int32)
    pos_keys = first_pos - SPAN * tok_rows + jnp.arange((SPAN + 1) * tok_rows, dtype=jnp.int32)
    return attend_window(query_proj, key_win, value_win, segment_ids, seg_win, pos_query, pos_keys)


def solution(mesh):
    return jax.shard_map(
        shards,
        mesh=mesh,
        in_specs=(
            P(("grp", "cp"), None),
            P(("grp", "cp"), None),
            P(("grp", "cp"), None),
            P(("grp", "cp")),
        ),
        out_specs=P(("grp", "cp"), None),
        check_vma=False,
    )
```

profile of v0, /device:TPU:32, one launch (start us, length us, event | category | flops | bytes accessed | tf_op | source)
XLA Modules:
  0.0 327.8 jit_solution(9573968862798963156)
XLA Ops:
  0.0 2.0 collective-permute-start.1
  2.1 4.9 %collective-permute-start = (s32[128]{0:T(128)}, s32[128]{0:T(128)S(1)}, u32[]{:S(2)}, u32[]{:S(2)}) collective-permute-start(s32[128]{0:T(128)} %param.7), channel_id=1, source_target_pairs={{0,8},{1,9},{2,10},{3,11},{4,12},{5,13},{6,14},{7,15},{8,16},{9,17... | collective-permute-start | bytes 1544 | tf_op jit(solution)/shard_map/ppermute | solution.py:15
  7.0 1.0 copy.28
  8.0 27.9 %collective-permute-start.9 = (bf16[128,512]{0,1:T(8,128)(2,1)S(1)}, bf16[128,512]{0,1:T(8,128)(2,1)S(1)}, u32[]{:S(2)}, u32[]{:S(2)}) collective-permute-start(bf16[128,512]{0,1:T(8,128)(2,1)S(1)} %copy.28), channel_id=1, source_target_pairs={{0,1},{1,2},{2,3},{3,4},{4,5},{5,6},{6,7},{7,8},{8,9},{9,10},{10,1... | collective-permute-start | bytes 393224 | tf_op jit(solution)/shard_map/ppermute | solution.py:15
  35.9 3.4 %collective-permute-start.8 = (bf16[128,512]{0,1:T(8,128)(2,1)S(1)}, bf16[128,512]{0,1:T(8,128)(2,1)S(1)}, u32[]{:S(2)}, u32[]{:S(2)}) collective-permute-start(bf16[128,512]{0,1:T(8,128)(2,1)S(1)} %copy.28), channel_id=1, source_target_pairs={{0,8},{1,9},{2,10},{3,11},{4,12},{5,13},{6,14},{7,15},{8,16},{9,17... | collective-permute-start | bytes 393224 | tf_op jit(solution)/shard_map/ppermute | solution.py:15
  39.4 1.9 collective-permute-start.5
  41.3 1.4 fusion.104
  42.8 8.8 %collective-permute-start.2 = (s32[256]{0:T(256)S(1)}, s32[256]{0:T(256)S(1)}, u32[]{:S(2)}, u32[]{:S(2)}) collective-permute-start(s32[256]{0:T(256)S(1)} %pad_add_fusion.1), channel_id=1, source_target_pairs={{0,2},{1,3},{2,4},{3,5},{4,6},{5,7},{6,8},{7,9},{8,10},{9,11},{10,... | collective-permute-start | bytes 3080 | tf_op jit(solution)/shard_map/ppermute | solution.py:15
  51.6 0.1 copy.86
  51.7 0.1 copy.85
  51.8 0.1 copy.84
  52.0 0.1 copy.83
  52.1 0.1 copy.82
  52.2 0.1 copy.81
  52.4 0.1 copy.80
  52.5 0.1 copy.79
  52.6 33.8 %collective-permute-done.2 = s32[256]{0:T(256)S(1)} collective-permute-done((s32[256]{0:T(256)S(1)}, s32[256]{0:T(256)S(1)}, u32[]{:S(2)}, u32[]{:S(2)}) %collective-permute-start.2) | collective-permute-done | bytes 1056 | tf_op jit(solution)/shard_map/ppermute | solution.py:15
  86.4 1.9 collective-permute-start.4
  88.4 1.9 collective-permute-start.3
  90.3 7.8 %collective-permute-done.3 = s32[512]{0:T(512)S(1)} collective-permute-done((s32[512]{0:T(512)S(1)}, s32[512]{0:T(512)S(1)}, u32[]{:S(2)}, u32[]{:S(2)}) %collective-permute-start.3) | collective-permute-done | bytes 2080 | tf_op jit(solution)/shard_map/ppermute | solution.py:15
  98.2 1.9 collective-permute-start.6
  100.2 17.8 %collective-permute-start.10 = (bf16[256,512]{0,1:T(8,128)(2,1)S(1)}, bf16[256,512]{0,1:T(8,128)(2,1)S(1)}, u32[]{:S(2)}, u32[]{:S(2)}) collective-permute-start(bf16[256,512]{0,1:T(8,128)(2,1)S(1)} %pad_maximum_fusion.2), channel_id=1, source_target_pairs={{0,2},{1,3},{2,4},{3,5},{4,6},{5,7},{6,8},{7,9},{8,10},{9,11},{10,... | collective-permute-start | bytes 786440 | tf_op jit(solution)/shard_map/ppermute | solution.py:15
  118.0 157.7 %collective-permute-done.6 = bf16[256,512]{1,0:T(8,128)(2,1)S(1)} collective-permute-done((bf16[256,512]{1,0:T(8,128)(2,1)S(1)}, bf16[256,512]{1,0:T(8,128)(2,1)S(1)}, u32[]{:S(2)}, u32[]{:S(2)}) %collective-permute-start.6) | collective-permute-done | bytes 262176 | tf_op jit(solution)/shard_map/ppermute | solution.py:15
  275.7 1.9 collective-permute-start.7
  277.7 1.1 and_and_fusion
  278.8 2.5 collective-permute-done.10
  281.3 2.1 collective-permute-start.11
  283.5 13.2 %collective-permute-done.7 = bf16[512,512]{1,0:T(8,128)(2,1)S(1)} collective-permute-done((bf16[512,512]{1,0:T(8,128)(2,1)S(1)}, bf16[512,512]{1,0:T(8,128)(2,1)S(1)}, u32[]{:S(2)}, u32[]{:S(2)}) %collective-permute-start.7) | collective-permute-done | bytes 524320 | tf_op jit(solution)/shard_map/ppermute | solution.py:15
  296.7 10.2 %collective-permute-done.11 = bf16[512,512]{0,1:T(8,128)(2,1)S(1)} collective-permute-done((bf16[512,512]{0,1:T(8,128)(2,1)S(1)}, bf16[512,512]{0,1:T(8,128)(2,1)S(1)}, u32[]{:S(2)}, u32[]{:S(2)}) %collective-permute-start.11) | collective-permute-done | bytes 524320 | tf_op jit(solution)/shard_map/ppermute | solution.py:15
  307.1 0.5 fusion.105
  307.5 0.3 fusion.16
  307.9 0.2 copy-done.1
  308.1 0.5 fusion.101
  308.7 0.7 constant_dynamic-update-slice_fusion.18
  309.4 0.5 fusion.106
  309.9 0.3 fusion.18
  310.2 1.5 fusion.98
  311.9 0.5 fusion.107
  312.3 0.3 fusion.20
  312.7 1.5 fusion.95
  314.3 0.5 fusion.108
  314.8 0.3 fusion.22
  315.1 1.5 fusion.92
  316.8 0.5 fusion.109
  317.2 0.3 fusion.24
  317.6 0.5 copy-done.2
  318.0 0.6 fusion.89
  318.7 0.5 fusion.110
  319.2 0.3 fusion.26
  319.5 0.6 fusion.86
  320.2 0.5 fusion.111
  320.7 0.3 fusion.28
  321.0 0.6 fusion.83
  321.7 0.5 fusion.112
  322.2 0.3 fusion.30
  322.5 0.6 fusion.80
  323.1 0.1 copy.62
  323.2 0.7 constant_dynamic-update-slice_fusion.17
  323.8 0.7 constant_dynamic-update-slice_fusion.16
  324.5 0.7 constant_dynamic-update-slice_fusion.15
  325.2 0.7 constant_dynamic-update-slice_fusion.14
  325.8 0.7 constant_dynamic-update-slice_fusion.13
  326.5 0.7 constant_dynamic-update-slice_fusion.12
  327.2 0.7 constant_dynamic-update-slice_fusion.11
  (44 shorter events, 1.2 us)
Async XLA Ops:
  0.0 42.7 %copy-start.3 = (s32[128]{0:T(128)S(1)}, s32[128]{0:T(128)}, u32[]{:S(2)}) copy-start(s32[128]{0:T(128)} %param.7) | copy-start | bytes 1540
  0.0 86.4 %copy-start = (bf16[128,512]{1,0:T(8,128)(2,1)S(1)}, bf16[128,512]{1,0:T(8,128)(2,1)}, u32[]{:S(2)}) copy-start(bf16[128,512]{1,0:T(8,128)(2,1)} %param.5) | copy-start | bytes 393220
  0.0 42.7 %collective-permute-start.1 = (s32[128]{0:T(128)}, s32[128]{0:T(128)S(1)}, u32[]{:S(2)}, u32[]{:S(2)}) collective-permute-start(s32[128]{0:T(128)} %param.7), channel_id=1, source_target_pairs={{0,1},{1,2},{2,3},{3,4},{4,5},{5,6},{6,7},{7,8},{8,9},{9,10},{10,1... | collective-permute-start | bytes 1544 | tf_op jit(solution)/shard_map/ppermute | solution.py:15
  2.1 86.3 %collective-permute-start = (s32[128]{0:T(128)}, s32[128]{0:T(128)S(1)}, u32[]{:S(2)}, u32[]{:S(2)}) collective-permute-start(s32[128]{0:T(128)} %param.7), channel_id=1, source_target_pairs={{0,8},{1,9},{2,10},{3,11},{4,12},{5,13},{6,14},{7,15},{8,16},{9,17... | collective-permute-start | bytes 1544 | tf_op jit(solution)/shard_map/ppermute | solution.py:15
  8.0 92.1 %collective-permute-start.9 = (bf16[128,512]{0,1:T(8,128)(2,1)S(1)}, bf16[128,512]{0,1:T(8,128)(2,1)S(1)}, u32[]{:S(2)}, u32[]{:S(2)}) collective-permute-start(bf16[128,512]{0,1:T(8,128)(2,1)S(1)} %copy.28), channel_id=1, source_target_pairs={{0,1},{1,2},{2,3},{3,4},{4,5},{5,6},{6,7},{7,8},{8,9},{9,10},{10,1... | collective-permute-start | bytes 393224 | tf_op jit(solution)/shard_map/ppermute | solution.py:15
  35.9 247.5 %collective-permute-start.8 = (bf16[128,512]{0,1:T(8,128)(2,1)S(1)}, bf16[128,512]{0,1:T(8,128)(2,1)S(1)}, u32[]{:S(2)}, u32[]{:S(2)}) collective-permute-start(bf16[128,512]{0,1:T(8,128)(2,1)S(1)} %copy.28), channel_id=1, source_target_pairs={{0,8},{1,9},{2,10},{3,11},{4,12},{5,13},{6,14},{7,15},{8,16},{9,17... | collective-permute-start | bytes 393224 | tf_op jit(solution)/shard_map/ppermute | solution.py:15
  39.4 58.8 %collective-permute-start.5 = (bf16[128,512]{1,0:T(8,128)(2,1)}, bf16[128,512]{1,0:T(8,128)(2,1)S(1)}, u32[]{:S(2)}, u32[]{:S(2)}) collective-permute-start(bf16[128,512]{1,0:T(8,128)(2,1)} %param.5), channel_id=1, source_target_pairs={{0,1},{1,2},{2,3},{3,4},{4,5},{5,6},{6,7},{7,8},{8,9},{9,10},{10,1... | collective-permute-start | bytes 393224 | tf_op jit(solution)/shard_map/ppermute | solution.py:15
  42.8 43.7 %collective-permute-start.2 = (s32[256]{0:T(256)S(1)}, s32[256]{0:T(256)S(1)}, u32[]{:S(2)}, u32[]{:S(2)}) collective-permute-start(s32[256]{0:T(256)S(1)} %pad_add_fusion.1), channel_id=1, source_target_pairs={{0,2},{1,3},{2,4},{3,5},{4,6},{5,7},{6,8},{7,9},{8,10},{9,11},{10,... | collective-permute-start | bytes 3080 | tf_op jit(solution)/shard_map/ppermute | solution.py:15
  86.4 192.3 %collective-permute-start.4 = (bf16[128,512]{1,0:T(8,128)(2,1)S(1)}, bf16[128,512]{1,0:T(8,128)(2,1)S(1)}, u32[]{:S(2)}, u32[]{:S(2)}) collective-permute-start(bf16[128,512]{1,0:T(8,128)(2,1)S(1)} %copy-done), channel_id=1, source_target_pairs={{0,8},{1,9},{2,10},{3,11},{4,12},{5,13},{6,14},{7,15},{8,16},{9,17... | collective-permute-start | bytes 393224 | tf_op jit(solution)/shard_map/ppermute | solution.py:15
  88.4 9.7 %collective-permute-start.3 = (s32[512]{0:T(512)S(1)}, s32[512]{0:T(512)S(1)}, u32[]{:S(2)}, u32[]{:S(2)}) collective-permute-start(s32[512]{0:T(512)S(1)} %pad_add_fusion), channel_id=1, source_target_pairs={{0,4},{1,5},{2,6},{3,7},{4,8},{5,9},{6,10},{7,11},{8,12},{9,13},{1... | collective-permute-start | bytes 6152 | tf_op jit(solution)/shard_map/ppermute | solution.py:15
  98.2 177.5 %collective-permute-start.6 = (bf16[256,512]{1,0:T(8,128)(2,1)S(1)}, bf16[256,512]{1,0:T(8,128)(2,1)S(1)}, u32[]{:S(2)}, u32[]{:S(2)}) collective-permute-start(bf16[256,512]{1,0:T(8,128)(2,1)S(1)} %pad_maximum_fusion.3), channel_id=1, source_target_pairs={{0,2},{1,3},{2,4},{3,5},{4,6},{5,7},{6,8},{7,9},{8,10},{9,11},{10,... | collective-permute-start | bytes 786440 | tf_op jit(solution)/shard_map/ppermute | solution.py:15
  100.2 181.1 %collective-permute-start.10 = (bf16[256,512]{0,1:T(8,128)(2,1)S(1)}, bf16[256,512]{0,1:T(8,128)(2,1)S(1)}, u32[]{:S(2)}, u32[]{:S(2)}) collective-permute-start(bf16[256,512]{0,1:T(8,128)(2,1)S(1)} %pad_maximum_fusion.2), channel_id=1, source_target_pairs={{0,2},{1,3},{2,4},{3,5},{4,6},{5,7},{6,8},{7,9},{8,10},{9,11},{10,... | collective-permute-start | bytes 786440 | tf_op jit(solution)/shard_map/ppermute | solution.py:15
  275.7 20.9 %collective-permute-start.7 = (bf16[512,512]{1,0:T(8,128)(2,1)S(1)}, bf16[512,512]{1,0:T(8,128)(2,1)S(1)}, u32[]{:S(2)}, u32[]{:S(2)}) collective-permute-start(bf16[512,512]{1,0:T(8,128)(2,1)S(1)} %pad_maximum_fusion.1), channel_id=1, source_target_pairs={{0,4},{1,5},{2,6},{3,7},{4,8},{5,9},{6,10},{7,11},{8,12},{9,13},{1... | collective-permute-start | bytes 1572872 | tf_op jit(solution)/shard_map/ppermute | solution.py:15
  281.3 25.6 %collective-permute-start.11 = (bf16[512,512]{0,1:T(8,128)(2,1)S(1)}, bf16[512,512]{0,1:T(8,128)(2,1)S(1)}, u32[]{:S(2)}, u32[]{:S(2)}) collective-permute-start(bf16[512,512]{0,1:T(8,128)(2,1)S(1)} %pad_maximum_fusion), channel_id=1, source_target_pairs={{0,4},{1,5},{2,6},{3,7},{4,8},{5,9},{6,10},{7,11},{8,12},{9,13},{1... | collective-permute-start | bytes 1572872 | tf_op jit(solution)/shard_map/ppermute | solution.py:15
  307.1 1.0 copy-start.1
  316.8 1.3 copy-start.2
where the time goes:
time: 328 us
  waiting for transfers between devices  225 us (69%)
  starting transfers between devices  76.6 us (23%)
  matrix products  11.1 us (3%)
  local copies, waits for them, and re-layouts  10.5 us (3%)
  other arithmetic  3.91 us (1%)
    ppermute x12, waiting for transfers between devices, passed_along(): lax.ppermute(value, axis, [(source, source + steps) for source in range(f...  225 us
    ppermute x12, starting transfers between devices, passed_along(): lax.ppermute(value, axis, [(source, source + steps) for source in range(f...  76.6 us
    unnamed x36, local copies, waits for them, and re-layouts  7.51 us
    dot_general x8, matrix products, attend_window(): jnp.einsum('tgs,sd->tgd', probs, v_block, preferred_element_type=jnp.floa...  7.34 us
  transfers between devices with their start and end apart: 12, of which 6 were waited for; matrix products, arithmetic and copies ran while one was open for 1% of the time, Pallas kernels for 0%

commit v1 on v0

v1 whole, which is shorter than its diff:
```python
import functools
import math

import jax
import jax.numpy as jnp
from jax import lax
from jax.experimental import pallas as pl
from jax.experimental.pallas import tpu as pltpu
from jax.sharding import PartitionSpec as P

HEAD = 128
META = 8
AXES = ("grp", "cp")
HIDDEN = -1e30
STACK = 4


def moved(value, target):
    count = lax.axis_size(AXES)
    pairs = [(s, target(s)) for s in range(count)]
    return lax.ppermute(value, AXES, [(s, t) for s, t in pairs if t is not None and 0 <= t < count])


def doc_rows(segments, width):
    ids = (segments + 1)[None, :]
    row = lax.broadcasted_iota(jnp.int32, (META, ids.shape[1]), 0)
    digits = jnp.where(row == 0, ids // 256, jnp.where(row == 1, ids % 256, 0)).astype(jnp.bfloat16)
    return jnp.pad(digits, ((0, 0), (0, width - digits.shape[1])))


def doc_line(rows):
    return rows[0:1, :].astype(jnp.float32) * 256.0 + rows[1:2, :].astype(jnp.float32)


def attend(heads, q_ref, own_docs, packs, docs, before, outs):
    tok = q_ref.shape[0]
    mine = jnp.broadcast_to(own_docs, (tok, tok)).T
    tiles = [mine == jnp.broadcast_to(d, (tok, tok)) for d in docs]
    if not before:
        rows = lax.broadcasted_iota(jnp.int32, (tok, tok), 0)
        cols = lax.broadcasted_iota(jnp.int32, (tok, tok), 1)
        tiles[0] = tiles[0] & (cols <= rows)
    mask = jnp.concatenate([jnp.concatenate(tiles, 1)] * STACK, 0)
    keys = jnp.concatenate([p[0:tok, :] for p in packs], 0)
    values = jnp.concatenate([p[tok : 2 * tok, :] for p in packs], 0)
    to_base_two = math.log2(math.e) / math.sqrt(HEAD)
    full = (STACK * tok, HEAD)
    for start in range(0, heads, STACK):
        rows = slice(start * tok, (start + STACK) * tok)
        queries = jnp.concatenate([q_ref[:, i * HEAD : (i + 1) * HEAD] for i in range(start, start + STACK)], 0)
        scores = lax.dot_general(queries, keys, (((1,), (1,)), ((), ())), preferred_element_type=jnp.float32)
        scores = jnp.where(mask, scores * to_base_two, HIDDEN)
        top = jnp.broadcast_to(jnp.max(scores, axis=1, keepdims=True), full)
        if before:
            old = before[1][0, rows, :]
            top = jnp.maximum(top, old)
        weights = jnp.exp2(scores - jnp.concatenate([top] * len(packs), 1))
        total = jnp.broadcast_to(jnp.sum(weights, axis=1, keepdims=True), full)
        mixed = jnp.dot(weights.astype(jnp.bfloat16), values, preferred_element_type=jnp.float32)
        if before:
            share = jnp.exp2(old - top)
            mixed = (mixed + before[0][0, rows, :] * share) * (1.0 / (total + share))
            for i in range(STACK):
                outs[0][:, (start + i) * HEAD : (start + i + 1) * HEAD] = mixed[i * tok : (i + 1) * tok].astype(jnp.bfloat16)
        else:
            outs[0][0, rows, :] = mixed * (1.0 / total)
            outs[1][0, rows, :] = top + jnp.log2(total)


def near_kernel(heads, q, p0, p1, p2, p3, p4, d0, d1, d2, d3, d4, *outs):
    docs = [doc_line(d[...]) for d in (d0, d1, d2, d3, d4)]
    attend(heads, q, docs[0], [p[...] for p in (p0, p1, p2, p3, p4)], docs, (), outs)


def far_kernel(heads, flag, q, own, p0, right, p1, p2, p3, d0, d_right, d1, d2, d3, mixed, logs, *outs):
    put_right = flag[0] > 0
    docs = [jnp.where(put_right, doc_line(d_right[...]), doc_line(d0[...]))] + [doc_line(d[...]) for d in (d1, d2, d3)]
    packs = [jnp.where(put_right, right[...], p0[...])] + [p[...] for p in (p1, p2, p3)]
    attend(heads, q, doc_line(own[...]), packs, docs, (mixed, logs), outs)


def shards(query_proj, key_proj, value_projection, segment_ids):
    tok, width = query_proj.shape
    kv = key_proj.shape[1] // HEAD
    heads = width // HEAD // kv
    group = lax.axis_size("cp")
    place = lax.axis_index("cp")
    odd = place % 2 == 1
    opening = place < 4
    closing = place >= group - 4
    partner = lambda s: s ^ 1

    own = jnp.concatenate([key_proj, value_projection, doc_rows(segment_ids, key_proj.shape[1])], 0)

    def over(s):
        return s + 4 if s % group >= group - 4 else s + 4 + group if s % group >= group - 8 else None

    outside = moved(own, over)
    crossed = moved(own, lambda s: s // group * group + (s + 2) % group)
    round_four = moved(jnp.where(closing, outside, own), lambda s: s // group * group + (s + 4) % group)
    four = jnp.where(opening, outside, round_four)
    eight = moved(four, lambda s: s + 4 if s % group < group - 4 else None)
    eight = jnp.where(opening, round_four, eight)
    four_there = moved(four, partner)
    rest_there = moved(jnp.where(odd, eight, own), partner)
    near = [own, four, eight, four_there, rest_there]

    tall = jax.ShapeDtypeStruct((kv, heads * tok, HEAD), jnp.float32)
    slab = pl.BlockSpec((1, heads * tok, HEAD), lambda h: (h, 0, 0))
    pack = pl.BlockSpec((2 * tok + META, HEAD), lambda h: (0, h))
    docs = pl.BlockSpec((META, HEAD), lambda h: (2 * tok // META, 0))
    query = pl.BlockSpec((tok, heads * HEAD), lambda h: (0, h))
    flag = pl.BlockSpec(memory_space=pltpu.SMEM)

    def call(kernel, shard_count, in_specs, final=False):
        return pl.pallas_call(
            functools.partial(kernel, heads),
            grid=(kv,),
            in_specs=in_specs,
            out_specs=query if final else [slab] * 2,
            out_shape=jax.ShapeDtypeStruct((tok, width), jnp.bfloat16) if final else [tall] * 2,
            compiler_params=pltpu.CompilerParams(dimension_semantics=("arbitrary",), vmem_limit_bytes=20 << 20),
            cost_estimate=pl.CostEstimate(
                flops=shard_count * 4 * tok * tok * HEAD * heads * kv, bytes_accessed=9 << 20, transcendentals=0
            ),
        )

    mixed, logs = call(near_kernel, 5, [query] + [pack] * 5 + [docs] * 5)(query_proj, *near, *near)

    turned = lambda s: group if s % group < 2 else 0
    crossed, mixed, logs, query_late, own_late = lax.optimization_barrier((crossed, mixed, logs, query_proj, own))
    onward = moved(crossed, lambda s: s + 4 + turned(s))
    put_right = moved(crossed, lambda s: s + group if s % group < 2 else None)
    crossed_there = moved(crossed, lambda s: (s ^ 1) + turned(s))
    onward_there = moved(onward, partner)
    first = (place < 2).astype(jnp.int32).reshape(1)
    far = [crossed, put_right, crossed_there, onward, onward_there]
    return call(far_kernel, 4, [flag, query, docs] + [pack] * 5 + [docs] * 5 + [slab] * 2, True)(
        first, query_late, own_late, *far, *far, mixed, logs
    )


def solution(mesh):
    return jax.shard_map(
        shards,
        mesh=mesh,
        in_specs=(P(AXES, None), P(AXES, None), P(AXES, None), P(AXES)),
        out_specs=P(AXES, None),
        check_vma=False,
    )
```

time: 328 us -> 146 us (0.45)
  waiting for transfers between devices: 225 us -> 77.6 us
  starting transfers between devices: 76.6 us -> 46 us
  Pallas kernels: 0 us -> 12.8 us
  matrix products: 11.1 us -> 0 us
  local copies, waits for them, and re-layouts: 10.5 us -> 6.33 us
    ppermute x12 -> x10, waiting for transfers between devices: 225 us -> 77.6 us  [moved(): lax.ppermute(value, AXES, [(s, t) for s, t in pairs if t is not None and...]
    ppermute x12 -> x10, starting transfers between devices: 76.6 us -> 46 us  [moved(): lax.ppermute(value, AXES, [(s, t) for s, t in pairs if t is not None and...]
    pallas_call x0 -> x2, Pallas kernels: none -> 12.8 us  [the longest x1 6.56 us: shards(): call(near_kernel, 5, [query] + [pack] * 5 + [docs] * 5)]
    dot_general x16 -> x0, matrix products: 11.1 us -> none  [the longest x8 7.34 us: attend_window(): jnp.einsum('tgs,sd->tgd', probs, v_block, preferred_element_type=jnp.floa...]
    unnamed x36 -> x16, local copies, waits for them, and re-layouts: 7.51 us -> 6.33 us
  transfers between devices with their start and end apart: 12 -> 10, of which waited for: 6 -> 7; matrix products, arithmetic and copies ran while one was open for 1% -> 0% of each run, Pallas kernels for 0% -> 4%
where the time goes in v1:
time: 146 us
  waiting for transfers between devices  77.6 us (53%)
  starting transfers between devices  46 us (32%)
  Pallas kernels  12.8 us (9%)
  local copies, waits for them, and re-layouts  6.33 us (4%)
  other arithmetic  2.99 us (2%)
    ppermute x10, waiting for transfers between devices, moved(): lax.ppermute(value, AXES, [(s, t) for s, t in pairs if t is not None and...  77.6 us
    ppermute x10, starting transfers between devices, moved(): lax.ppermute(value, AXES, [(s, t) for s, t in pairs if t is not None and...  46 us
    pallas_call x1, Pallas kernels, shards(): call(near_kernel, 5, [query] + [pack] * 5 + [docs] * 5)  6.56 us
    unnamed x16, local copies, waits for them, and re-layouts  6.33 us
    pallas_call x1, Pallas kernels, shards(): call(far_kernel, 4, [flag, query, docs] + [pack] * 5 + [docs] * 5 + [slab...  6.28 us
  transfers between devices with their start and end apart: 10, of which 7 were waited for; matrix products, arithmetic and copies ran while one was open for 0% of the time, Pallas kernels for 4%

profile of v1, /device:TPU:32, one launch (start us, length us, event | category | flops | bytes accessed | tf_op | source)
XLA Modules:
  0.0 145.9 jit_solution(5188625387403763992)
XLA Ops:
  0.0 0.0 copy-start.6
  0.0 0.0 copy-start.7
  0.0 0.7 and_select_fusion.1
  0.7 0.1 select_convert_fusion
  0.8 1.0 fusion.1.p0.d0.own
  1.8 0.0 copy-start.2
  1.8 1.3 collective-permute-start.1
  3.1 13.0 %collective-permute-done.1 = bf16[264,512]{1,0:T(8,128)(2,1)S(1)} collective-permute-done((bf16[264,512]{1,0:T(8,128)(2,1)S(1)}, bf16[264,512]{1,0:T(8,128)(2,1)S(1)}, u32[]{:S(2)}, u32[]{:S(2)}) %collective-permute-start.1) | collective-permute-done | bytes 270368 | tf_op jit(solution)/shard_map/ppermute | solution.py:21
  16.1 1.1 broadcast_select_fusion.1
  17.2 1.9 %collective-permute-start.2 = (bf16[264,512]{1,0:T(8,128)(2,1)S(1)}, bf16[264,512]{1,0:T(8,128)(2,1)S(1)}, u32[]{:S(2)}, u32[]{:S(2)}) collective-permute-start(bf16[264,512]{1,0:T(8,128)(2,1)S(1)} %broadcast_select_fusion.1), channel_id=1, source_target_pairs={{0,4},{1,5},{2,6},{3,7},{4,8},{5,9},{6,10},{7,11},{8,12},{9,13},{1... | collective-permute-start | bytes 811016 | tf_op jit(solution)/shard_map/ppermute | solution.py:21
  19.1 10.6 %collective-permute-done.2 = bf16[264,512]{1,0:T(8,128)(2,1)S(1)} collective-permute-done((bf16[264,512]{1,0:T(8,128)(2,1)S(1)}, bf16[264,512]{1,0:T(8,128)(2,1)S(1)}, u32[]{:S(2)}, u32[]{:S(2)}) %collective-permute-start.2) | collective-permute-done | bytes 270368 | tf_op jit(solution)/shard_map/ppermute | solution.py:21
  29.8 1.3 collective-permute-start.3
  31.1 1.9 %collective-permute-start.4 = (bf16[264,512]{1,0:T(8,128)(2,1)S(1)}, bf16[264,512]{1,0:T(8,128)(2,1)S(1)}, u32[]{:S(2)}, u32[]{:S(2)}) collective-permute-start(bf16[264,512]{1,0:T(8,128)(2,1)S(1)} %broadcast_select_fusion.3.p1.d1), channel_id=1, source_target_pairs={{0,1},{1,0},{2,3},{3,2},{4,5},{5,4},{6,7},{7,6},{8,9},{9,8},{10,11... | collective-permute-start | bytes 811016 | tf_op jit(solution)/shard_map/ppermute | solution.py:21
  33.1 2.3 %collective-permute-done.3 = bf16[264,512]{1,0:T(8,128)(2,1)S(1)} collective-permute-done((bf16[264,512]{1,0:T(8,128)(2,1)S(1)}, bf16[264,512]{1,0:T(8,128)(2,1)S(1)}, u32[]{:S(2)}, u32[]{:S(2)}) %collective-permute-start.3) | collective-permute-done | bytes 270368 | tf_op jit(solution)/shard_map/ppermute | solution.py:21
  35.4 0.0 copy-done.6
  35.4 0.0 copy-done.7
  35.4 0.1 broadcast_select_fusion
  35.5 1.9 %collective-permute-start.5 = (bf16[264,512]{1,0:T(8,128)(2,1)S(1)}, bf16[264,512]{1,0:T(8,128)(2,1)S(1)}, u32[]{:S(2)}, u32[]{:S(2)}) collective-permute-start(bf16[264,512]{1,0:T(8,128)(2,1)S(1)} %get-tuple-element.19), channel_id=1, source_target_pairs={{0,1},{1,0},{2,3},{3,2},{4,5},{5,4},{6,7},{7,6},{8,9},{9,8},{10,11... | collective-permute-start | bytes 811016 | tf_op jit(solution)/shard_map/ppermute | solution.py:21
  37.5 28.1 %collective-permute-start = (bf16[264,512]{1,0:T(8,128)(2,1)S(1)}, bf16[264,512]{1,0:T(8,128)(2,1)S(1)}, u32[]{:S(2)}, u32[]{:S(2)}) collective-permute-start(bf16[264,512]{1,0:T(8,128)(2,1)S(1)} %fusion.1.p0.d0.own), channel_id=1, source_target_pairs={{0,2},{1,3},{2,4},{3,5},{4,6},{5,7},{6,8},{7,9},{8,10},{9,11},{10,... | collective-permute-start | bytes 811016 | tf_op jit(solution)/shard_map/ppermute | solution.py:21
  65.5 0.0 collective-permute-done.4.p3.d3
  65.6 0.0 collective-permute-done.5.p4.d4
  65.6 0.0 copy-start.4
  65.6 1.2 copy-done.4
  66.8 6.6 %shard_map.46 = (f32[4,1024,128]{2,1,0:T(8,128)S(1)}, f32[4,1024,128]{2,1,0:T(8,128)S(1)}) custom-call(bf16[128,4096]{1,0:T(8,128)(2,1)S(1)} %copy-done.4, bf16[264,512]{1,0:T(8,128)(2,1)S(1)} %fusion.1.p0.d0.own, bf16[264,512]{1,0:T(8,128)(2,1)S(1)} %broadcast_select_fusion.3.p1.d1, bf16[264,512]{1,0:T(8,128)(2,1)S(1)} %get-tuple-element.20.p2.d2, ...), custom_call_target="tpu_custom_call" | custom-call | flops 1342177280 | bytes 9437184 | tf_op jit(solution)/shard_map/pallas_call | solution.py:128
  73.4 0.0 copy-done.2
  73.4 0.0 copy-start
  73.4 1.3 copy-done
  74.7 36.2 %collective-permute-done.p0.d0 = bf16[264,512]{1,0:T(8,128)(2,1)S(1)} collective-permute-done((bf16[264,512]{1,0:T(8,128)(2,1)S(1)}, bf16[264,512]{1,0:T(8,128)(2,1)S(1)}, u32[]{:S(2)}, u32[]{:S(2)}) %collective-permute-start) | collective-permute-done | bytes 270368 | tf_op jit(solution)/shard_map/ppermute | solution.py:21
  110.9 1.9 %collective-permute-start.8 = (bf16[264,512]{1,0:T(8,128)(2,1)S(1)}, bf16[264,512]{1,0:T(8,128)(2,1)S(1)}, u32[]{:S(2)}, u32[]{:S(2)}) collective-permute-start(bf16[264,512]{1,0:T(8,128)(2,1)S(1)} %collective-permute-done.p0.d0), channel_id=1, source_target_pairs={{0,68},{1,69},{2,6},{3,7},{4,8},{5,9},{6,10},{7,11},{8,12},{9,13},... | collective-permute-start | bytes 811016 | tf_op jit(solution)/shard_map/ppermute | solution.py:21
  112.9 2.8 %collective-permute-start.7 = (bf16[264,512]{1,0:T(8,128)(2,1)S(1)}, bf16[264,512]{1,0:T(8,128)(2,1)S(1)}, u32[]{:S(2)}, u32[]{:S(2)}) collective-permute-start(bf16[264,512]{1,0:T(8,128)(2,1)S(1)} %collective-permute-done.p0.d0), channel_id=1, source_target_pairs={{0,65},{1,64},{2,3},{3,2},{4,5},{5,4},{6,7},{7,6},{8,9},{9,8},{10,... | collective-permute-start | bytes 811016 | tf_op jit(solution)/shard_map/ppermute | solution.py:21
  115.7 3.0 %collective-permute-start.6 = (bf16[264,512]{1,0:T(8,128)(2,1)S(1)}, bf16[264,512]{1,0:T(8,128)(2,1)S(1)}, u32[]{:S(2)}, u32[]{:S(2)}) collective-permute-start(bf16[264,512]{1,0:T(8,128)(2,1)S(1)} %collective-permute-done.p0.d0), channel_id=1, source_target_pairs={{0,64},{1,65},{64,128},{65,129},{128,192},{129,193},{192,256},{193... | collective-permute-start | bytes 811016 | tf_op jit(solution)/shard_map/ppermute | solution.py:21
  118.7 6.1 %collective-permute-done.8.p2.d2 = bf16[264,512]{1,0:T(8,128)(2,1)S(1)} collective-permute-done((bf16[264,512]{1,0:T(8,128)(2,1)S(1)}, bf16[264,512]{1,0:T(8,128)(2,1)S(1)}, u32[]{:S(2)}, u32[]{:S(2)}) %collective-permute-start.8) | collective-permute-done | bytes 270368 | tf_op jit(solution)/shard_map/ppermute | solution.py:21
  124.7 1.9 %collective-permute-start.9 = (bf16[264,512]{1,0:T(8,128)(2,1)S(1)}, bf16[264,512]{1,0:T(8,128)(2,1)S(1)}, u32[]{:S(2)}, u32[]{:S(2)}) collective-permute-start(bf16[264,512]{1,0:T(8,128)(2,1)S(1)} %collective-permute-done.8.p2.d2), channel_id=1, source_target_pairs={{0,1},{1,0},{2,3},{3,2},{4,5},{5,4},{6,7},{7,6},{8,9},{9,8},{10,11... | collective-permute-start | bytes 811016 | tf_op jit(solution)/shard_map/ppermute | solution.py:21
  126.6 2.1 %collective-permute-done.7.p1.d1 = bf16[264,512]{1,0:T(8,128)(2,1)S(1)} collective-permute-done((bf16[264,512]{1,0:T(8,128)(2,1)S(1)}, bf16[264,512]{1,0:T(8,128)(2,1)S(1)}, u32[]{:S(2)}, u32[]{:S(2)}) %collective-permute-start.7) | collective-permute-done | bytes 270368 | tf_op jit(solution)/shard_map/ppermute | solution.py:21
  128.8 7.1 %collective-permute-done.6.right.d_right = bf16[264,512]{1,0:T(8,128)(2,1)S(1)} collective-permute-done((bf16[264,512]{1,0:T(8,128)(2,1)S(1)}, bf16[264,512]{1,0:T(8,128)(2,1)S(1)}, u32[]{:S(2)}, u32[]{:S(2)}) %collective-permute-start.6) | collective-permute-done | bytes 270368 | tf_op jit(solution)/shard_map/ppermute | solution.py:21
  135.9 0.0 collective-permute-done.9.p3.d3
  135.9 0.0 copy-start.1
  135.9 1.6 %copy-done.1 = f32[4,1024,128]{2,1,0:T(8,128)S(1)} copy-done((f32[4,1024,128]{2,1,0:T(8,128)S(1)}, f32[4,1024,128]{2,1,0:T(8,128)}, u32[]{:S(2)}) %copy-start.1) | copy-done | bytes 2097176
  137.5 0.0 copy-start.3
  137.5 1.0 copy-done.3
  138.4 0.0 copy-start.5
  138.4 1.2 copy-done.5
  139.7 6.3 %shard_map.47 = bf16[128,4096]{1,0:T(8,128)(2,1)} custom-call(s32[1]{0:T(128)} %bitcast.flag, bf16[128,4096]{1,0:T(8,128)(2,1)S(1)} %copy-done.5, bf16[264,512]{1,0:T(8,128)(2,1)S(1)} %copy-done.3, bf16[264,512]{1,0:T(8,128)(2,1)S(1)} %collective-permute-done.p0.d0, bf16[264,512]{1,0:T(8,128)(2,1)S(1)} %collective-permute-done.6.right.d_right, ...), custom_call_target="tpu_custom_call" | custom-call | flops 1073741824 | bytes 9437184 | tf_op jit(solution)/shard_map/pallas_call | solution.py:138
  (3 shorter events, 0.0 us)
Async XLA Ops:
  0.0 35.4 %copy-start.6 = (bf16[128,512]{1,0:T(8,128)(2,1)S(1)}, bf16[128,512]{1,0:T(8,128)(2,1)}, u32[]{:S(2)}) copy-start(bf16[128,512]{1,0:T(8,128)(2,1)} %param.6) | copy-start | bytes 393220
  0.0 35.4 %copy-start.7 = (bf16[128,512]{1,0:T(8,128)(2,1)S(1)}, bf16[128,512]{1,0:T(8,128)(2,1)}, u32[]{:S(2)}) copy-start(bf16[128,512]{1,0:T(8,128)(2,1)} %param.5) | copy-start | bytes 393220
  1.8 71.6 %copy-start.2 = (bf16[264,512]{1,0:T(8,128)(2,1)}, bf16[264,512]{1,0:T(8,128)(2,1)S(1)}, u32[]{:S(2)}) copy-start(bf16[264,512]{1,0:T(8,128)(2,1)S(1)} %fusion.1.p0.d0.own) | copy-start | bytes 811012
  1.8 14.3 %collective-permute-start.1 = (bf16[264,512]{1,0:T(8,128)(2,1)S(1)}, bf16[264,512]{1,0:T(8,128)(2,1)S(1)}, u32[]{:S(2)}, u32[]{:S(2)}) collective-permute-start(bf16[264,512]{1,0:T(8,128)(2,1)S(1)} %fusion.1.p0.d0.own), channel_id=1, source_target_pairs={{56,124},{57,125},{58,126},{59,127},{60,64},{61,65},{62,66},{63,67... | collective-permute-start | bytes 811016 | tf_op jit(solution)/shard_map/ppermute | solution.py:21
  17.2 12.6 %collective-permute-start.2 = (bf16[264,512]{1,0:T(8,128)(2,1)S(1)}, bf16[264,512]{1,0:T(8,128)(2,1)S(1)}, u32[]{:S(2)}, u32[]{:S(2)}) collective-permute-start(bf16[264,512]{1,0:T(8,128)(2,1)S(1)} %broadcast_select_fusion.1), channel_id=1, source_target_pairs={{0,4},{1,5},{2,6},{3,7},{4,8},{5,9},{6,10},{7,11},{8,12},{9,13},{1... | collective-permute-start | bytes 811016 | tf_op jit(solution)/shard_map/ppermute | solution.py:21
  29.8 5.6 %collective-permute-start.3 = (bf16[264,512]{1,0:T(8,128)(2,1)S(1)}, bf16[264,512]{1,0:T(8,128)(2,1)S(1)}, u32[]{:S(2)}, u32[]{:S(2)}) collective-permute-start(bf16[264,512]{1,0:T(8,128)(2,1)S(1)} %broadcast_select_fusion.3.p1.d1), channel_id=1, source_target_pairs={{0,4},{1,5},{2,6},{3,7},{4,8},{5,9},{6,10},{7,11},{8,12},{9,13},{1... | collective-permute-start | bytes 811016 | tf_op jit(solution)/shard_map/ppermute | solution.py:21
  31.1 34.4 %collective-permute-start.4 = (bf16[264,512]{1,0:T(8,128)(2,1)S(1)}, bf16[264,512]{1,0:T(8,128)(2,1)S(1)}, u32[]{:S(2)}, u32[]{:S(2)}) collective-permute-start(bf16[264,512]{1,0:T(8,128)(2,1)S(1)} %broadcast_select_fusion.3.p1.d1), channel_id=1, source_target_pairs={{0,1},{1,0},{2,3},{3,2},{4,5},{5,4},{6,7},{7,6},{8,9},{9,8},{10,11... | collective-permute-start | bytes 811016 | tf_op jit(solution)/shard_map/ppermute | solution.py:21
  35.5 30.0 %collective-permute-start.5 = (bf16[264,512]{1,0:T(8,128)(2,1)S(1)}, bf16[264,512]{1,0:T(8,128)(2,1)S(1)}, u32[]{:S(2)}, u32[]{:S(2)}) collective-permute-start(bf16[264,512]{1,0:T(8,128)(2,1)S(1)} %get-tuple-element.19), channel_id=1, source_target_pairs={{0,1},{1,0},{2,3},{3,2},{4,5},{5,4},{6,7},{7,6},{8,9},{9,8},{10,11... | collective-permute-start | bytes 811016 | tf_op jit(solution)/shard_map/ppermute | solution.py:21
  37.5 73.5 %collective-permute-start = (bf16[264,512]{1,0:T(8,128)(2,1)S(1)}, bf16[264,512]{1,0:T(8,128)(2,1)S(1)}, u32[]{:S(2)}, u32[]{:S(2)}) collective-permute-start(bf16[264,512]{1,0:T(8,128)(2,1)S(1)} %fusion.1.p0.d0.own), channel_id=1, source_target_pairs={{0,2},{1,3},{2,4},{3,5},{4,6},{5,7},{6,8},{7,9},{8,10},{9,11},{10,... | collective-permute-start | bytes 811016 | tf_op jit(solution)/shard_map/ppermute | solution.py:21
  65.6 1.2 copy-start.4
  73.4 1.3 copy-start
  110.9 13.8 %collective-permute-start.8 = (bf16[264,512]{1,0:T(8,128)(2,1)S(1)}, bf16[264,512]{1,0:T(8,128)(2,1)S(1)}, u32[]{:S(2)}, u32[]{:S(2)}) collective-permute-start(bf16[264,512]{1,0:T(8,128)(2,1)S(1)} %collective-permute-done.p0.d0), channel_id=1, source_target_pairs={{0,68},{1,69},{2,6},{3,7},{4,8},{5,9},{6,10},{7,11},{8,12},{9,13},... | collective-permute-start | bytes 811016 | tf_op jit(solution)/shard_map/ppermute | solution.py:21
  112.9 15.9 %collective-permute-start.7 = (bf16[264,512]{1,0:T(8,128)(2,1)S(1)}, bf16[264,512]{1,0:T(8,128)(2,1)S(1)}, u32[]{:S(2)}, u32[]{:S(2)}) collective-permute-start(bf16[264,512]{1,0:T(8,128)(2,1)S(1)} %collective-permute-done.p0.d0), channel_id=1, source_target_pairs={{0,65},{1,64},{2,3},{3,2},{4,5},{5,4},{6,7},{7,6},{8,9},{9,8},{10,... | collective-permute-start | bytes 811016 | tf_op jit(solution)/shard_map/ppermute | solution.py:21
  115.7 20.2 %collective-permute-start.6 = (bf16[264,512]{1,0:T(8,128)(2,1)S(1)}, bf16[264,512]{1,0:T(8,128)(2,1)S(1)}, u32[]{:S(2)}, u32[]{:S(2)}) collective-permute-start(bf16[264,512]{1,0:T(8,128)(2,1)S(1)} %collective-permute-done.p0.d0), channel_id=1, source_target_pairs={{0,64},{1,65},{64,128},{65,129},{128,192},{129,193},{192,256},{193... | collective-permute-start | bytes 811016 | tf_op jit(solution)/shard_map/ppermute | solution.py:21
  124.7 11.2 %collective-permute-start.9 = (bf16[264,512]{1,0:T(8,128)(2,1)S(1)}, bf16[264,512]{1,0:T(8,128)(2,1)S(1)}, u32[]{:S(2)}, u32[]{:S(2)}) collective-permute-start(bf16[264,512]{1,0:T(8,128)(2,1)S(1)} %collective-permute-done.8.p2.d2), channel_id=1, source_target_pairs={{0,1},{1,0},{2,3},{3,2},{4,5},{5,4},{6,7},{7,6},{8,9},{9,8},{10,11... | collective-permute-start | bytes 811016 | tf_op jit(solution)/shard_map/ppermute | solution.py:21
  135.9 1.6 %copy-start.1 = (f32[4,1024,128]{2,1,0:T(8,128)S(1)}, f32[4,1024,128]{2,1,0:T(8,128)}, u32[]{:S(2)}) copy-start(f32[4,1024,128]{2,1,0:T(8,128)} %copy-done) | copy-start | bytes 6291460
  137.5 1.0 copy-start.3
  138.4 1.2 copy-start.5

commit v2 on v1

--- a/solution.py
+++ b/solution.py
@@ -72,11 +72,9 @@
     attend(heads, q, docs[0], [p[...] for p in (p0, p1, p2, p3, p4)], docs, (), outs)
 
 
-def far_kernel(heads, flag, q, own, p0, right, p1, p2, p3, d0, d_right, d1, d2, d3, mixed, logs, *outs):
-    put_right = flag[0] > 0
-    docs = [jnp.where(put_right, doc_line(d_right[...]), doc_line(d0[...]))] + [doc_line(d[...]) for d in (d1, d2, d3)]
-    packs = [jnp.where(put_right, right[...], p0[...])] + [p[...] for p in (p1, p2, p3)]
-    attend(heads, q, doc_line(own[...]), packs, docs, (mixed, logs), outs)
+def far_kernel(heads, q, own, p0, p1, p2, p3, d0, d1, d2, d3, mixed, logs, *outs):
+    docs = [doc_line(d[...]) for d in (d0, d1, d2, d3)]
+    attend(heads, q, doc_line(own[...]), [p[...] for p in (p0, p1, p2, p3)], docs, (mixed, logs), outs)
 
 
 def shards(query_proj, key_proj, value_projection, segment_ids):
@@ -127,16 +125,15 @@
 
     mixed, logs = call(near_kernel, 5, [query] + [pack] * 5 + [docs] * 5)(query_proj, *near, *near)
 
-    turned = lambda s: group if s % group < 2 else 0
-    crossed, mixed, logs, query_late, own_late = lax.optimization_barrier((crossed, mixed, logs, query_proj, own))
-    onward = moved(crossed, lambda s: s + 4 + turned(s))
+    crossed, mixed = lax.optimization_barrier((crossed, mixed))
+    onward = moved(crossed, lambda s: s + 4 + (group if s % group < 2 else 0))
     put_right = moved(crossed, lambda s: s + group if s % group < 2 else None)
-    crossed_there = moved(crossed, lambda s: (s ^ 1) + turned(s))
+    crossed = jnp.where(place < 2, put_right, crossed)
+    crossed_there = moved(crossed, partner)
     onward_there = moved(onward, partner)
-    first = (place < 2).astype(jnp.int32).reshape(1)
-    far = [crossed, put_right, crossed_there, onward, onward_there]
-    return call(far_kernel, 4, [flag, query, docs] + [pack] * 5 + [docs] * 5 + [slab] * 2, True)(
-        first, query_late, own_late, *far, *far, mixed, logs
+    far = [crossed, crossed_there, onward, onward_there]
+    return call(far_kernel, 4, [query, docs] + [pack] * 4 + [docs] * 4 + [slab] * 2, True)(
+        query_proj, own, *far, *far, mixed, logs
     )
 
 

time: 146 us -> 144 us (0.986)
  the two profiles are of different devices: /device:TPU:32 before, /device:TPU:1 now
where the time goes in v2:
time: 144 us; the launch traced here: 143 us
  starting transfers between devices  99 us (69%)
  waiting for transfers between devices  22.8 us (16%)
  Pallas kernels  12.8 us (9%)
  local copies, waits for them, and re-layouts  5.38 us (4%)
  other arithmetic  3.03 us (2%)
    ppermute x10, starting transfers between devices, moved(): lax.ppermute(value, AXES, [(s, t) for s, t in pairs if t is not None and...  99 us
    ppermute x10, waiting for transfers between devices, moved(): lax.ppermute(value, AXES, [(s, t) for s, t in pairs if t is not None and...  22.8 us
    pallas_call x1, Pallas kernels, shards(): call(near_kernel, 5, [query] + [pack] * 5 + [docs] * 5)  6.56 us
    pallas_call x1, Pallas kernels, shards(): call(far_kernel, 4, [query, docs] + [pack] * 4 + [docs] * 4 + [slab] * 2,...  6.23 us
    unnamed x12, local copies, waits for them, and re-layouts  5.38 us
  transfers between devices with their start and end apart: 10, of which 5 were waited for; matrix products, arithmetic and copies ran while one was open for 0% of the time, Pallas kernels for 5%

profile of v2, /device:TPU:1, one launch (start us, length us, event | category | flops | bytes accessed | tf_op | source)
XLA Modules:
  0.0 143.2 jit_solution(6160271940276252792)
XLA Ops:
  0.0 0.0 copy-start.4
  0.0 0.0 copy-start.5
  0.0 0.7 and_select_fusion.1
  0.7 0.1 select_convert_fusion
  0.8 1.0 fusion.1.p0.d0.own
  1.8 0.7 collective-permute-start.1
  2.5 0.0 collective-permute-done.1
  2.5 1.1 broadcast_select_fusion.1
  3.6 3.9 %collective-permute-start.2 = (bf16[264,512]{1,0:T(8,128)(2,1)S(1)}, bf16[264,512]{1,0:T(8,128)(2,1)S(1)}, u32[]{:S(2)}, u32[]{:S(2)}) collective-permute-start(bf16[264,512]{1,0:T(8,128)(2,1)S(1)} %broadcast_select_fusion.1), channel_id=1, source_target_pairs={{0,4},{1,5},{2,6},{3,7},{4,8},{5,9},{6,10},{7,11},{8,12},{9,13},{1... | collective-permute-start | bytes 811016 | tf_op jit(solution)/shard_map/ppermute | solution.py:21
  7.5 15.1 %collective-permute-done.2 = bf16[264,512]{1,0:T(8,128)(2,1)S(1)} collective-permute-done((bf16[264,512]{1,0:T(8,128)(2,1)S(1)}, bf16[264,512]{1,0:T(8,128)(2,1)S(1)}, u32[]{:S(2)}, u32[]{:S(2)}) %collective-permute-start.2) | collective-permute-done | bytes 270368 | tf_op jit(solution)/shard_map/ppermute | solution.py:21
  22.7 1.3 collective-permute-start.3
  24.0 8.6 %collective-permute-start.4 = (bf16[264,512]{1,0:T(8,128)(2,1)S(1)}, bf16[264,512]{1,0:T(8,128)(2,1)S(1)}, u32[]{:S(2)}, u32[]{:S(2)}) collective-permute-start(bf16[264,512]{1,0:T(8,128)(2,1)S(1)} %broadcast_select_fusion.3.p1.d1), channel_id=1, source_target_pairs={{0,1},{1,0},{2,3},{3,2},{4,5},{5,4},{6,7},{7,6},{8,9},{9,8},{10,11... | collective-permute-start | bytes 811016 | tf_op jit(solution)/shard_map/ppermute | solution.py:21
  32.6 0.0 collective-permute-done.3
  32.6 0.0 copy-done.4
  32.6 0.0 copy-done.5
  32.7 0.1 broadcast_select_fusion
  32.8 3.9 %collective-permute-start.5 = (bf16[264,512]{1,0:T(8,128)(2,1)S(1)}, bf16[264,512]{1,0:T(8,128)(2,1)S(1)}, u32[]{:S(2)}, u32[]{:S(2)}) collective-permute-start(bf16[264,512]{1,0:T(8,128)(2,1)S(1)} %get-tuple-element.13), channel_id=1, source_target_pairs={{0,1},{1,0},{2,3},{3,2},{4,5},{5,4},{6,7},{7,6},{8,9},{9,8},{10,11... | collective-permute-start | bytes 811016 | tf_op jit(solution)/shard_map/ppermute | solution.py:21
  36.7 25.3 %collective-permute-start = (bf16[264,512]{1,0:T(8,128)(2,1)S(1)}, bf16[264,512]{1,0:T(8,128)(2,1)S(1)}, u32[]{:S(2)}, u32[]{:S(2)}) collective-permute-start(bf16[264,512]{1,0:T(8,128)(2,1)S(1)} %fusion.1.p0.d0.own), channel_id=1, source_target_pairs={{0,2},{1,3},{2,4},{3,5},{4,6},{5,7},{6,8},{7,9},{8,10},{9,11},{10,... | collective-permute-start | bytes 811016 | tf_op jit(solution)/shard_map/ppermute | solution.py:21
  62.0 0.0 collective-permute-done.4.p3.d3
  62.0 0.0 collective-permute-done.5.p4.d4
  62.0 0.0 copy-start.2
  62.0 1.2 copy-done.2
  63.2 6.6 %shard_map.46 = (f32[4,1024,128]{2,1,0:T(8,128)S(1)}, f32[4,1024,128]{2,1,0:T(8,128)S(1)}) custom-call(bf16[128,4096]{1,0:T(8,128)(2,1)S(1)} %copy-done.2, bf16[264,512]{1,0:T(8,128)(2,1)S(1)} %fusion.1.p0.d0.own, bf16[264,512]{1,0:T(8,128)(2,1)S(1)} %broadcast_select_fusion.3.p1.d1, bf16[264,512]{1,0:T(8,128)(2,1)S(1)} %get-tuple-element.14.p2.d2, ...), custom_call_target="tpu_custom_call" | custom-call | flops 1342177280 | bytes 9437184 | tf_op jit(solution)/shard_map/pallas_call | solution.py:126
  69.8 0.0 copy-start
  69.8 1.3 copy-done
  71.1 2.0 %collective-permute-done = bf16[264,512]{1,0:T(8,128)(2,1)S(1)} collective-permute-done((bf16[264,512]{1,0:T(8,128)(2,1)S(1)}, bf16[264,512]{1,0:T(8,128)(2,1)S(1)}, u32[]{:S(2)}, u32[]{:S(2)}) %collective-permute-start) | collective-permute-done | bytes 270368 | tf_op jit(solution)/shard_map/ppermute | solution.py:21
  73.2 45.4 %collective-permute-start.8 = (bf16[264,512]{1,0:T(8,128)(2,1)S(1)}, bf16[264,512]{1,0:T(8,128)(2,1)S(1)}, u32[]{:S(2)}, u32[]{:S(2)}) collective-permute-start(bf16[264,512]{1,0:T(8,128)(2,1)S(1)} %collective-permute-done), channel_id=1, source_target_pairs={{0,68},{1,69},{2,6},{3,7},{4,8},{5,9},{6,10},{7,11},{8,12},{9,13},... | collective-permute-start | bytes 811016 | tf_op jit(solution)/shard_map/ppermute | solution.py:21
  118.6 1.3 collective-permute-start.6
  119.9 3.6 %collective-permute-done.8.p2.d2 = bf16[264,512]{1,0:T(8,128)(2,1)S(1)} collective-permute-done((bf16[264,512]{1,0:T(8,128)(2,1)S(1)}, bf16[264,512]{1,0:T(8,128)(2,1)S(1)}, u32[]{:S(2)}, u32[]{:S(2)}) %collective-permute-start.8) | collective-permute-done | bytes 270368 | tf_op jit(solution)/shard_map/ppermute | solution.py:21
  123.5 5.0 %collective-permute-start.9 = (bf16[264,512]{1,0:T(8,128)(2,1)S(1)}, bf16[264,512]{1,0:T(8,128)(2,1)S(1)}, u32[]{:S(2)}, u32[]{:S(2)}) collective-permute-start(bf16[264,512]{1,0:T(8,128)(2,1)S(1)} %collective-permute-done.8.p2.d2), channel_id=1, source_target_pairs={{0,1},{1,0},{2,3},{3,2},{4,5},{5,4},{6,7},{7,6},{8,9},{9,8},{10,11... | collective-permute-start | bytes 811016 | tf_op jit(solution)/shard_map/ppermute | solution.py:21
  128.5 0.8 collective-permute-done.6
  129.3 3.6 %collective-permute-start.7 = (bf16[264,512]{1,0:T(8,128)(2,1)S(1)}, bf16[264,512]{1,0:T(8,128)(2,1)S(1)}, u32[]{:S(2)}, u32[]{:S(2)}) collective-permute-start(bf16[264,512]{1,0:T(8,128)(2,1)S(1)} %broadcast_select_fusion.4.p0.d0), channel_id=1, source_target_pairs={{0,1},{1,0},{2,3},{3,2},{4,5},{5,4},{6,7},{7,6},{8,9},{9,8},{10,11... | collective-permute-start | bytes 811016 | tf_op jit(solution)/shard_map/ppermute | solution.py:21
  133.0 0.0 collective-permute-done.9.p3.d3
  133.0 1.1 collective-permute-done.7.p1.d1
  134.1 0.0 copy-start.1
  134.1 1.6 %copy-done.1 = f32[4,1024,128]{2,1,0:T(8,128)S(1)} copy-done((f32[4,1024,128]{2,1,0:T(8,128)S(1)}, f32[4,1024,128]{2,1,0:T(8,128)}, u32[]{:S(2)}) %copy-start.1) | copy-done | bytes 2097176
  135.7 0.0 copy-start.3
  135.7 1.2 copy-done.3
  136.9 6.2 %shard_map.47 = bf16[128,4096]{1,0:T(8,128)(2,1)} custom-call(bf16[128,4096]{1,0:T(8,128)(2,1)S(1)} %copy-done.3, bf16[264,512]{1,0:T(8,128)(2,1)S(1)} %fusion.1.p0.d0.own, bf16[264,512]{1,0:T(8,128)(2,1)S(1)} %broadcast_select_fusion.4.p0.d0, bf16[264,512]{1,0:T(8,128)(2,1)S(1)} %collective-permute-done.7.p1.d1, ...), custom_call_target="tpu_custom_call" | custom-call | flops 1073741824 | bytes 9437184 | tf_op jit(solution)/shard_map/pallas_call | solution.py:135
  (4 shorter events, 0.1 us)
Async XLA Ops:
  0.0 32.6 %copy-start.4 = (bf16[128,512]{1,0:T(8,128)(2,1)S(1)}, bf16[128,512]{1,0:T(8,128)(2,1)}, u32[]{:S(2)}) copy-start(bf16[128,512]{1,0:T(8,128)(2,1)} %param.6) | copy-start | bytes 393220
  0.0 32.6 %copy-start.5 = (bf16[128,512]{1,0:T(8,128)(2,1)S(1)}, bf16[128,512]{1,0:T(8,128)(2,1)}, u32[]{:S(2)}) copy-start(bf16[128,512]{1,0:T(8,128)(2,1)} %param.5) | copy-start | bytes 393220
  1.8 0.7 collective-permute-start.1
  3.6 19.1 %collective-permute-start.2 = (bf16[264,512]{1,0:T(8,128)(2,1)S(1)}, bf16[264,512]{1,0:T(8,128)(2,1)S(1)}, u32[]{:S(2)}, u32[]{:S(2)}) collective-permute-start(bf16[264,512]{1,0:T(8,128)(2,1)S(1)} %broadcast_select_fusion.1), channel_id=1, source_target_pairs={{0,4},{1,5},{2,6},{3,7},{4,8},{5,9},{6,10},{7,11},{8,12},{9,13},{1... | collective-permute-start | bytes 811016 | tf_op jit(solution)/shard_map/ppermute | solution.py:21
  22.7 10.0 %collective-permute-start.3 = (bf16[264,512]{1,0:T(8,128)(2,1)S(1)}, bf16[264,512]{1,0:T(8,128)(2,1)S(1)}, u32[]{:S(2)}, u32[]{:S(2)}) collective-permute-start(bf16[264,512]{1,0:T(8,128)(2,1)S(1)} %broadcast_select_fusion.3.p1.d1), channel_id=1, source_target_pairs={{0,4},{1,5},{2,6},{3,7},{4,8},{5,9},{6,10},{7,11},{8,12},{9,13},{1... | collective-permute-start | bytes 811016 | tf_op jit(solution)/shard_map/ppermute | solution.py:21
  24.0 38.0 %collective-permute-start.4 = (bf16[264,512]{1,0:T(8,128)(2,1)S(1)}, bf16[264,512]{1,0:T(8,128)(2,1)S(1)}, u32[]{:S(2)}, u32[]{:S(2)}) collective-permute-start(bf16[264,512]{1,0:T(8,128)(2,1)S(1)} %broadcast_select_fusion.3.p1.d1), channel_id=1, source_target_pairs={{0,1},{1,0},{2,3},{3,2},{4,5},{5,4},{6,7},{7,6},{8,9},{9,8},{10,11... | collective-permute-start | bytes 811016 | tf_op jit(solution)/shard_map/ppermute | solution.py:21
  32.8 29.2 %collective-permute-start.5 = (bf16[264,512]{1,0:T(8,128)(2,1)S(1)}, bf16[264,512]{1,0:T(8,128)(2,1)S(1)}, u32[]{:S(2)}, u32[]{:S(2)}) collective-permute-start(bf16[264,512]{1,0:T(8,128)(2,1)S(1)} %get-tuple-element.13), channel_id=1, source_target_pairs={{0,1},{1,0},{2,3},{3,2},{4,5},{5,4},{6,7},{7,6},{8,9},{9,8},{10,11... | collective-permute-start | bytes 811016 | tf_op jit(solution)/shard_map/ppermute | solution.py:21
  36.7 36.5 %collective-permute-start = (bf16[264,512]{1,0:T(8,128)(2,1)S(1)}, bf16[264,512]{1,0:T(8,128)(2,1)S(1)}, u32[]{:S(2)}, u32[]{:S(2)}) collective-permute-start(bf16[264,512]{1,0:T(8,128)(2,1)S(1)} %fusion.1.p0.d0.own), channel_id=1, source_target_pairs={{0,2},{1,3},{2,4},{3,5},{4,6},{5,7},{6,8},{7,9},{8,10},{9,11},{10,... | collective-permute-start | bytes 811016 | tf_op jit(solution)/shard_map/ppermute | solution.py:21
  62.0 1.2 copy-start.2
  69.8 1.3 copy-start
  73.2 50.3 %collective-permute-start.8 = (bf16[264,512]{1,0:T(8,128)(2,1)S(1)}, bf16[264,512]{1,0:T(8,128)(2,1)S(1)}, u32[]{:S(2)}, u32[]{:S(2)}) collective-permute-start(bf16[264,512]{1,0:T(8,128)(2,1)S(1)} %collective-permute-done), channel_id=1, source_target_pairs={{0,68},{1,69},{2,6},{3,7},{4,8},{5,9},{6,10},{7,11},{8,12},{9,13},... | collective-permute-start | bytes 811016 | tf_op jit(solution)/shard_map/ppermute | solution.py:21
  118.6 10.7 %collective-permute-start.6 = (bf16[264,512]{1,0:T(8,128)(2,1)S(1)}, bf16[264,512]{1,0:T(8,128)(2,1)S(1)}, u32[]{:S(2)}, u32[]{:S(2)}) collective-permute-start(bf16[264,512]{1,0:T(8,128)(2,1)S(1)} %collective-permute-done), channel_id=1, source_target_pairs={{0,64},{1,65},{64,128},{65,129},{128,192},{129,193},{192,256},{193... | collective-permute-start | bytes 811016 | tf_op jit(solution)/shard_map/ppermute | solution.py:21
  123.5 9.5 %collective-permute-start.9 = (bf16[264,512]{1,0:T(8,128)(2,1)S(1)}, bf16[264,512]{1,0:T(8,128)(2,1)S(1)}, u32[]{:S(2)}, u32[]{:S(2)}) collective-permute-start(bf16[264,512]{1,0:T(8,128)(2,1)S(1)} %collective-permute-done.8.p2.d2), channel_id=1, source_target_pairs={{0,1},{1,0},{2,3},{3,2},{4,5},{5,4},{6,7},{7,6},{8,9},{9,8},{10,11... | collective-permute-start | bytes 811016 | tf_op jit(solution)/shard_map/ppermute | solution.py:21
  129.3 4.8 %collective-permute-start.7 = (bf16[264,512]{1,0:T(8,128)(2,1)S(1)}, bf16[264,512]{1,0:T(8,128)(2,1)S(1)}, u32[]{:S(2)}, u32[]{:S(2)}) collective-permute-start(bf16[264,512]{1,0:T(8,128)(2,1)S(1)} %broadcast_select_fusion.4.p0.d0), channel_id=1, source_target_pairs={{0,1},{1,0},{2,3},{3,2},{4,5},{5,4},{6,7},{7,6},{8,9},{9,8},{10,11... | collective-permute-start | bytes 811016 | tf_op jit(solution)/shard_map/ppermute | solution.py:21
  134.1 1.6 %copy-start.1 = (f32[4,1024,128]{2,1,0:T(8,128)S(1)}, f32[4,1024,128]{2,1,0:T(8,128)}, u32[]{:S(2)}) copy-start(f32[4,1024,128]{2,1,0:T(8,128)} %copy-done) | copy-start | bytes 6291460
  135.7 1.2 copy-start.3
